TPU v7x, 32 devices: a whole 2x2x4 slice. The times are simulated.
32 devices in a mesh: grp: 2 (over y), ctx: 4 (over z), sub: 4 (over x, core).
Axes of the slice: x: 2, y: 2, z: 4, core: 2. Of those that a mesh axis runs over, the one named last changes fastest.
Arguments:
- queries: bfloat16 [64, 3072], P(('grp', 'ctx'), 'sub'), parts along dimension 0, may hold values from -1024 to 1024
- latent_cache: bfloat16 [3072, 576], P(('grp', 'ctx')), parts along dimension 0, may hold values from -8 to 8
- cache_len: int32 [8], P(('grp', 'ctx')), parts along dimension 0, may hold values from 16 to 384, as said below
- kv_up: bfloat16 [32, 256, 512], P(('grp', 'sub'), None, 'ctx'), parts along dimension 0, may hold values from -1 to 1
- o_weight: bfloat16 [2048, 2048], P('sub', 'ctx'), may hold values from -0.5 to 0.5
- residual: bfloat16 [64, 2048], P(('grp', 'ctx')), parts along dimension 0, may hold values from -3 to 3
- norm_gain: bfloat16 [2048], replicated, may hold values from 0.25 to 1.75
- route_ids: int32 [64, 6], P(('grp', 'ctx')), parts along dimension 0, may hold values from 0 to 63, all different within a row; in each aligned block of 8 rows (0 to 7, 8 to 15, ...) at most 2 rows name the same one
- route_weights: float32 [64, 6], P(('grp', 'ctx')), parts along dimension 0, may hold values from 0.1 to 0.6
- w_gate: bfloat16 [64, 2048, 1408], P('ctx', None, 'sub'), may hold values from -0.125 to 0.125
- w_up: bfloat16 [64, 2048, 1408], P('ctx', None, 'sub'), may hold values from -0.125 to 0.125
- w_down: bfloat16 [64, 1408, 2048], P('ctx', 'sub'), may hold values from -0.15625 to 0.15625
Outputs:
- layer_out: bfloat16 [64, 2048], P(('grp', 'ctx'), 'sub'), parts along dimension 0
There are 2 independent parts, one for each index of `grp`. A program takes and returns all parts, laid end to end along the dimension named above; an argument that names none is the same for every part. Nothing has to cross between parts.
Inputs may be any that keep to these rules, and one draw needn't show every extreme that they name: `route_ids`: each row names 6 different experts. Among the 8 rows of one ctx index no expert is named more than 2 times, and in every draw some expert is named exactly 2 times by the rows of some ctx index. cache_len[c] positions at the start of shard c are live; at least one shard is full.
All inputs are finite; a program needn't handle non-finite values.
Results may differ from a plain program's by a relative error of at most 0.015.
Values may be sent and summed in bfloat16 or wider, within the bound.
A program may use at most 128 MiB of HBM per device.

v0:
```python
import functools

import jax
import jax.numpy as jnp
from jax import lax
from jax.experimental import pallas as pl
from jax.experimental.pallas import tpu as pltpu
from jax.sharding import PartitionSpec as P

D = 2048
NOPE = 128
ROPE = 64
VDIM = 128
LATENT = 512
TOP = 6
CAP = 2


epsilon = 1e-06


def local_attention(absorbed, cache_rows, length, up_value):
    scores = jnp.einsum("qhc,kc->qhk", absorbed, cache_rows, preferred_element_type=jnp.float32) * (
        NOPE + ROPE
    ) ** (-0.5)
    live_mask = lax.broadcasted_iota(jnp.int32, (cache_rows.shape[0],), 0) < length
    scores = jnp.where(live_mask[None, None, :], scores, -jnp.inf)
    highest = jnp.max(scores, axis=2)
    weights = jnp.exp(scores - highest[:, :, None]).astype(jnp.bfloat16)
    totals = jnp.sum(weights, axis=2, dtype=jnp.float32)
    latent_out = jnp.einsum(
        "qhk,kl->qhl", weights, cache_rows[:, :LATENT], preferred_element_type=jnp.float32
    ).astype(jnp.bfloat16)
    head_out = jnp.einsum("qhl,hvl->qhv", latent_out, up_value, preferred_element_type=jnp.float32)
    return (highest, totals, head_out)


def body(
    queries,
    latent_cache,
    cache_len,
    kv_up,
    o_weight,
    residual,
    norm_gain,
    route_ids,
    route_weights,
    w_gate,
    w_up,
    w_down,
):
    ctx_count = lax.axis_size("ctx")
    sub_count = lax.axis_size("sub")
    heads_dev = kv_up.shape[0]
    token_count = queries.shape[0]
    up_full = lax.all_gather(kv_up, "ctx", axis=2, tiled=True)
    up_key = up_full[:, :NOPE, :]
    up_value = up_full[:, NOPE:, :]
    own_rows = queries.reshape(token_count, heads_dev, NOPE + ROPE)
    query_latent = jnp.einsum(
        "qhn,hnl->qhl", own_rows[:, :, :NOPE], up_key, preferred_element_type=jnp.float32
    ).astype(jnp.bfloat16)
    mine = jnp.concatenate([query_latent, own_rows[:, :, NOPE:]], axis=2).reshape(
        token_count, heads_dev * (LATENT + ROPE)
    )
    absorbed = lax.all_gather(mine, "ctx", axis=0, tiled=True).reshape(-1, heads_dev, LATENT + ROPE)
    highest, totals, head_out = local_attention(absorbed, latent_cache, cache_len[0], up_value)
    all_rows = absorbed.shape[0]
    got_out, got_high, got_total = (
        lax.all_to_all(
            head_out.reshape(all_rows, heads_dev * VDIM),
            "ctx",
            split_axis=0,
            concat_axis=0,
            tiled=True,
        ),
        lax.all_to_all(highest, "ctx", split_axis=0, concat_axis=0, tiled=True),
        lax.all_to_all(totals, "ctx", split_axis=0, concat_axis=0, tiled=True),
    )
    got_out = got_out.reshape(ctx_count, token_count, heads_dev, VDIM)
    got_high = got_high.reshape(ctx_count, token_count, heads_dev)
    got_total = got_total.reshape(ctx_count, token_count, heads_dev)
    overall = jnp.max(got_high, axis=0)
    factor = jnp.exp(got_high - overall[None])
    numerator = jnp.sum(got_out * factor[:, :, :, None], axis=0)
    denominator = jnp.sum(got_total * factor, axis=0)
    attention = (
        (numerator / denominator[:, :, None])
        .astype(jnp.bfloat16)
        .reshape(token_count, heads_dev * VDIM)
    )
    projected = jnp.dot(
        attention,
        lax.all_gather(o_weight, "ctx", axis=1, tiled=True),
        preferred_element_type=jnp.float32,
    )
    quarter = D // sub_count
    offset_cols = lax.axis_index("sub") * quarter
    hidden = residual.astype(jnp.float32) + lax.psum(projected.astype(jnp.bfloat16), "sub").astype(
        jnp.float32
    )
    inverse_rms = lax.rsqrt(jnp.mean(hidden * hidden, axis=1) + epsilon)
    normed = (hidden * inverse_rms[:, None] * norm_gain.astype(jnp.float32)).astype(jnp.bfloat16)
    hidden_part = lax.dynamic_slice_in_dim(hidden, offset_cols, quarter, 1)
    experts_dev = w_gate.shape[0]
    expert_total = experts_dev * ctx_count
    pair_count = token_count * TOP
    expert_ids = route_ids.reshape(pair_count)
    onehot = (expert_ids[:, None] == lax.broadcasted_iota(jnp.int32, (1, expert_total), 1)).astype(
        jnp.int32
    )
    earlier = jnp.cumsum(onehot, axis=0) - onehot
    slot_ids = jnp.sum(earlier * onehot, axis=1)
    targets = (expert_ids * CAP + slot_ids).reshape(token_count, TOP)
    matches = targets[:, :, None] == lax.broadcasted_iota(jnp.int32, (1, 1, expert_total * CAP), 2)
    select = jnp.sum(matches.astype(jnp.int32), axis=1).astype(jnp.bfloat16)
    outgoing = jnp.einsum("tj,td->jd", select, normed, preferred_element_type=jnp.float32).astype(
        jnp.bfloat16
    )
    outgoing = outgoing.reshape(ctx_count, experts_dev, CAP, D)
    received = lax.all_to_all(outgoing, "ctx", split_axis=0, concat_axis=0, tiled=True)
    gate_act = jnp.einsum("sekd,edf->sekf", received, w_gate, preferred_element_type=jnp.float32)
    up_act = jnp.einsum("sekd,edf->sekf", received, w_up, preferred_element_type=jnp.float32)
    gated_rows = (jax.nn.silu(gate_act) * up_act).astype(jnp.bfloat16)
    partial_out = jnp.einsum(
        "sekf,efd->sekd", gated_rows, w_down, preferred_element_type=jnp.float32
    )
    summed = lax.psum_scatter(
        partial_out.astype(jnp.bfloat16), "sub", scatter_dimension=3, tiled=True
    )
    back_rows = lax.all_to_all(summed, "ctx", split_axis=0, concat_axis=0, tiled=True)
    back_rows = back_rows.reshape(expert_total * CAP, quarter)
    mixing = jnp.sum(jnp.where(matches, route_weights[:, :, None], 0.0), axis=1)
    routed = jnp.dot(mixing, back_rows.astype(jnp.float32), precision=lax.Precision.HIGHEST)
    return (hidden_part + routed).astype(jnp.bfloat16)


LANES = 128
SLOTS = 12
MESH = pl.DeviceIdType.MESH
F32 = jnp.float32
BF16 = jnp.bfloat16


def fused_kernel(
    dims,
    q_ref,
    res_ref,
    ids_ref,
    mix_ref,
    live_ref,
    cache_ref,
    kv_ref,
    o_ref,
    gain_ref,
    gate_hbm,
    up_hbm,
    down_hbm,
    out_ref,
    q_all,
    res_all,
    comb_send,
    comb_all,
    ql_send,
    ql_all,
    lat_send,
    lat_all,
    stat_send,
    stat_all,
    att_send,
    att_all,
    proj_send,
    proj_all,
    hid_send,
    hid_all,
    normed,
    total,
    fin_send,
    fin_all,
    gate_buf,
    up_buf,
    down_buf,
    ctx_send,
    ctx_recv,
    sub_send,
    sub_recv,
    fin_ssem,
    fin_rsem,
    w_sem,
):
    ctx, sub, tok, heads, experts, slots = dims
    me_c = lax.axis_index("ctx")
    me_s = lax.axis_index("sub")
    span = ctx * tok
    rows = heads * span
    quarter = o_ref.shape[1]

    def weight_copies(e, slot):
        return (
            pltpu.make_async_copy(gate_hbm.at[e], gate_buf.at[slot], w_sem.at[slot, 0]),
            pltpu.make_async_copy(up_hbm.at[e], up_buf.at[slot], w_sem.at[slot, 1]),
            pltpu.make_async_copy(down_hbm.at[e], down_buf.at[slot], w_sem.at[slot, 2]),
        )

    def prefetch(e, carry):
        for copy in weight_copies(e, e):
            copy.start()
        return carry

    lax.fori_loop(0, slots, prefetch, 0)

    barrier = pltpu.get_barrier_semaphore()
    for dc in range(ctx):
        for ds in range(sub):
            if dc or ds:
                pl.semaphore_signal(
                    barrier,
                    inc=1,
                    device_id={"ctx": lax.rem(me_c + dc, ctx), "sub": lax.rem(me_s + ds, sub)},
                    device_id_type=MESH,
                )
    pl.semaphore_wait(barrier, ctx * sub - 1)

    def ctx_copy(phase, source_of, target, d):
        peer = lax.rem(me_c + d, ctx)
        return pltpu.make_async_remote_copy(
            src_ref=source_of(peer),
            dst_ref=target.at[me_c],
            send_sem=ctx_send.at[phase, d],
            recv_sem=ctx_recv.at[phase, d],
            device_id={"ctx": peer},
            device_id_type=MESH,
        )

    def ctx_start(phase, source_of, target):
        copies = [ctx_copy(phase, source_of, target, d) for d in range(1, ctx)]
        for copy in copies:
            copy.start()
        return copies

    def finish(copies):
        for copy in copies:
            copy.wait()

    def own_columns(peer):
        return pl.ds(pl.multiple_of(peer * quarter, quarter), quarter)

    copies = ctx_start(0, lambda peer: q_ref, q_all)
    early = ctx_start(6, lambda peer: res_ref.at[:, own_columns(peer)], res_all)
    q_all[me_c] = q_ref[...]
    res_all[me_c] = res_ref[:, own_columns(me_c)]
    lane = lax.broadcasted_iota(jnp.int32, (tok, LANES), 1)
    ids, mixes = ids_ref[...], mix_ref[...]
    for c in range(ctx):
        comb = jnp.zeros((tok, LANES), F32)
        for k in range(TOP):
            hit = (ids[:, k : k + 1] == lane + c * experts) & (lane < experts)
            comb += jnp.where(hit, mixes[:, k : k + 1], 0.0)
        comb_send[c] = comb
    early += ctx_start(7, lambda peer: comb_send.at[peer], comb_all)
    comb_all[me_c] = comb_send[me_c]
    finish(copies)

    per_head = NOPE + ROPE
    q_rows = q_all[...].astype(F32).reshape(span, heads * per_head)
    turned = [
        q_rows if h == 0 else pltpu.roll(q_rows, (heads - h) * per_head, 1) for h in range(heads)
    ]
    for h in range(heads):
        nope = turned[h][:, :NOPE].astype(BF16)
        part = jnp.dot(nope, kv_ref[h, :NOPE, :], preferred_element_type=F32).astype(BF16)
        ql_send[h * span : (h + 1) * span, :] = part
    copies = ctx_start(1, lambda peer: ql_send, ql_all)
    ql_all[me_c] = ql_send[...]
    rope = jnp.concatenate(
        [turned[h][:, NOPE:per_head] for h in range(heads)],
        axis=0,
    ).astype(BF16)
    nt = (((1,), (1,)), ((), ()))
    rope_scores = jnp.dot(rope, cache_ref[LATENT:, :], preferred_element_type=F32)
    finish(copies)
    lat_q = jnp.concatenate([ql_all[c] for c in range(ctx)], axis=1)
    scores = jnp.dot(lat_q, cache_ref[:LATENT, :], preferred_element_type=F32)
    scores = (scores + rope_scores) * (NOPE + ROPE) ** (-0.5)
    scores = jnp.where(live_ref[...] > 0.0, scores, -jnp.inf)
    highest = jnp.max(scores, axis=1, keepdims=True)
    weights = jnp.exp(scores - highest).astype(BF16)
    totals = jnp.sum(weights.astype(F32), axis=1, keepdims=True)
    lane = lax.broadcasted_iota(jnp.int32, (rows, LANES), 1)
    stats = jnp.where(lane < 64, highest, totals).T
    stat_send[0:8, :] = stats[0:8, :]
    stat_send[8:16, :] = stats[64:72, :]
    copies = ctx_start(3, lambda peer: stat_send, stat_all)
    stat_all[me_c] = stat_send[...]
    latent = lax.dot_general(
        weights, cache_ref[:LATENT, :], nt, preferred_element_type=F32
    ).astype(BF16)
    for c in range(ctx):
        lat_send[c] = latent[:, c * LANES : (c + 1) * LANES]
    copies += ctx_start(2, lambda peer: lat_send.at[peer], lat_all)
    lat_all[me_c] = lat_send[me_c]
    finish(copies)

    highs = [stat_all[c, 0:1, :] for c in range(ctx)]
    overall = functools.reduce(jnp.maximum, highs)
    factors = [jnp.exp(high - overall) for high in highs]
    denominator = sum(f * stat_all[c, 8:9, :] for c, f in enumerate(factors))
    merged = jnp.zeros((rows, LANES), F32)
    for c in range(ctx):
        scale = jnp.broadcast_to(factors[c] / denominator, (LANES, rows)).T
        merged += lat_all[c].astype(F32) * scale
    merged = merged.astype(BF16)
    for h in range(heads):
        part = lax.dot_general(
            merged[h * span : (h + 1) * span, :],
            kv_ref[h, NOPE:, :],
            nt,
            preferred_element_type=F32,
        )
        att_send[:, h * VDIM : (h + 1) * VDIM] = part.astype(BF16)
    copies = ctx_start(4, lambda peer: att_send, att_all)
    att_all[me_c] = att_send[...]
    finish(copies)
    attention = sum(att_all[c].astype(F32) for c in range(ctx)).astype(BF16)
    proj_send[...] = jnp.dot(attention, o_ref[...], preferred_element_type=F32).astype(BF16)
    copies = [
        pltpu.make_async_remote_copy(
            src_ref=proj_send,
            dst_ref=proj_all.at[me_s],
            send_sem=sub_send.at[d],
            recv_sem=sub_recv.at[d],
            device_id={"sub": lax.rem(me_s + d, sub)},
            device_id_type=MESH,
        )
        for d in range(1, sub)
    ]
    for copy in copies:
        copy.start()
    proj_all[me_s] = proj_send[...]
    finish(copies + early)
    residual = res_all[...].astype(F32).reshape(span, quarter)
    hid_send[...] = residual + sum(proj_all[s].astype(F32) for s in range(sub))
    copies = ctx_start(5, lambda peer: hid_send, hid_all)
    hid_all[me_c] = hid_send[...]
    finish(copies)

    squares = sum(
        jnp.sum(hid_all[c] * hid_all[c], axis=1, keepdims=True) for c in range(ctx)
    )
    inverse_rms = lax.rsqrt(squares / (ctx * quarter) + epsilon)
    for c in range(ctx):
        cols = slice(c * quarter, (c + 1) * quarter)
        normed[:, cols] = (hid_all[c] * inverse_rms * gain_ref[:, cols]).astype(BF16)

    total[...] = jnp.zeros_like(total)
    comb = comb_all[...].reshape(span, LANES)
    comb_lane = lax.broadcasted_iota(jnp.int32, (span, LANES), 1)

    def expert(e, carry):
        slot = lax.rem(e, slots)
        gate_copy, up_copy, down_copy = weight_copies(e, slot)
        gate_copy.wait()
        gate_act = lax.dot_general(normed[...], gate_buf[slot], nt, preferred_element_type=F32)
        up_copy.wait()
        up_act = lax.dot_general(normed[...], up_buf[slot], nt, preferred_element_type=F32)
        gated = (gate_act / (1.0 + jnp.exp(-gate_act)) * up_act).astype(BF16)
        down_copy.wait()
        mix = jnp.sum(jnp.where(comb_lane == e, comb, 0.0), axis=1, keepdims=True)
        total[...] += mix * jnp.dot(gated, down_buf[slot], preferred_element_type=F32)
        return carry

    def expert_and_refill(e, carry):
        expert(e, carry)
        for copy in weight_copies(e + slots, lax.rem(e, slots)):
            copy.start()
        return carry

    lax.fori_loop(0, experts - slots, expert_and_refill, 0)
    lax.fori_loop(experts - slots, experts, expert, 0)

    for c in range(ctx):
        for s in range(sub):
            fin_send[c * sub + s] = total[
                c * tok : (c + 1) * tok, s * quarter : (s + 1) * quarter
            ].astype(BF16)
    copies = []
    for dc in range(ctx):
        for ds in range(sub):
            if dc or ds:
                peer_c, peer_s = lax.rem(me_c + dc, ctx), lax.rem(me_s + ds, sub)
                copies.append(
                    pltpu.make_async_remote_copy(
                        src_ref=fin_send.at[peer_c * sub + peer_s],
                        dst_ref=fin_all.at[me_c * sub + me_s],
                        send_sem=fin_ssem.at[dc * sub + ds],
                        recv_sem=fin_rsem.at[dc * sub + ds],
                        device_id={"ctx": peer_c, "sub": peer_s},
                        device_id_type=MESH,
                    )
                )
                copies[-1].start()
    me = me_c * sub + me_s
    fin_all[me] = fin_send[me]
    hidden = hid_all[me_s, pl.ds(pl.multiple_of(me_c * tok, tok), tok), :]
    finish(copies)
    routed = sum(fin_all[i].astype(F32) for i in range(ctx * sub))
    out_ref[...] = (hidden + routed).astype(out_ref.dtype)


def fused_body(
    queries,
    latent_cache,
    cache_len,
    kv_up,
    o_weight,
    residual,
    norm_gain,
    route_ids,
    route_weights,
    w_gate,
    w_up,
    w_down,
):
    ctx, sub = lax.axis_size("ctx"), lax.axis_size("sub")
    heads, tok, experts = kv_up.shape[0], queries.shape[0], w_gate.shape[0]
    span, rows, quarter = ctx * tok, heads * ctx * tok, o_weight.shape[1]
    width = residual.shape[1]
    slots = min(SLOTS, experts)
    w_gate, w_up = jnp.swapaxes(w_gate, 1, 2), jnp.swapaxes(w_up, 1, 2)
    count = latent_cache.shape[0]
    live = (lax.broadcasted_iota(jnp.int32, (1, count), 1) < cache_len[0]).astype(F32)
    gain = norm_gain.astype(F32).reshape(1, width)
    vmem = pl.BlockSpec(memory_space=pltpu.VMEM)
    hbm = pl.BlockSpec(memory_space=pl.ANY)
    dma = pltpu.SemaphoreType.DMA
    return pl.pallas_call(
        functools.partial(fused_kernel, (ctx, sub, tok, heads, experts, slots)),
        out_shape=jax.ShapeDtypeStruct((tok, width // sub), BF16),
        in_specs=[vmem] * 9 + [hbm] * 3,
        out_specs=vmem,
        scratch_shapes=[
            pltpu.VMEM((ctx,) + queries.shape, BF16),
            pltpu.VMEM((ctx, tok, quarter), BF16),
            pltpu.VMEM((ctx, tok, LANES), F32),
            pltpu.VMEM((ctx, tok, LANES), F32),
            pltpu.VMEM((rows, LANES), BF16),
            pltpu.VMEM((ctx, rows, LANES), BF16),
            pltpu.VMEM((ctx, rows, LANES), BF16),
            pltpu.VMEM((ctx, rows, LANES), BF16),
            pltpu.VMEM((16, rows), F32),
            pltpu.VMEM((ctx, 16, rows), F32),
            pltpu.VMEM((span, heads * VDIM), BF16),
            pltpu.VMEM((ctx, span, heads * VDIM), BF16),
            pltpu.VMEM((span, quarter), BF16),
            pltpu.VMEM((sub, span, quarter), BF16),
            pltpu.VMEM((span, quarter), F32),
            pltpu.VMEM((ctx, span, quarter), F32),
            pltpu.VMEM((span, width), BF16),
            pltpu.VMEM((span, width), F32),
            pltpu.VMEM((ctx * sub, tok, quarter), BF16),
            pltpu.VMEM((ctx * sub, tok, quarter), BF16),
            pltpu.VMEM((slots,) + w_gate.shape[1:], BF16),
            pltpu.VMEM((slots,) + w_up.shape[1:], BF16),
            pltpu.VMEM((slots,) + w_down.shape[1:], BF16),
            dma((8, ctx)),
            dma((8, ctx)),
            dma((sub,)),
            dma((sub,)),
            dma((ctx * sub,)),
            dma((ctx * sub,)),
            dma((slots, 3)),
        ],
        compiler_params=pltpu.CompilerParams(
            collective_id=0, has_side_effects=True, vmem_limit_bytes=67043328
        ),
    )(
        queries,
        residual,
        route_ids,
        route_weights,
        live,
        latent_cache.T,
        kv_up,
        o_weight,
        gain,
        w_gate,
        w_up,
        w_down,
    )


def choose_body(*args):
    kv_up, o_weight, w_gate = args[3], args[4], args[9]
    ctx, sub, tok = lax.axis_size("ctx"), lax.axis_size("sub"), args[0].shape[0]
    fits = (
        ctx == sub
        and kv_up.shape[2] == LANES
        and o_weight.shape[1] % LANES == 0
        and kv_up.shape[0] * ctx * tok == LANES
        and w_gate.shape[0] <= LANES
        and tok % 8 == 0
    )
    return fused_body(*args) if fits else body(*args)


def solution(mesh):
    in_specs = (
        P(("grp", "ctx"), "sub"),
        P(("grp", "ctx"), None),
        P(("grp", "ctx")),
        P(("grp", "sub"), None, "ctx"),
        P("sub", "ctx"),
        P(("grp", "ctx"), None),
        P(),
        P(("grp", "ctx"), None),
        P(("grp", "ctx"), None),
        P("ctx", None, "sub"),
        P("ctx", None, "sub"),
        P("ctx", "sub", None),
    )
    out_specs = P(("grp", "ctx"), "sub")
    return jax.shard_map(choose_body, mesh=mesh, in_specs=in_specs, out_specs=out_specs, check_vma=False)
```

profile of v0, /device:TPU:0, one launch (start us, length us, event | category | flops | bytes accessed | tf_op | source)
XLA Modules:
  0.0 73.4 jit_solution(6907405602433030754)
XLA Ops:
  0.7 0.6 compare_convert_fusion.live_ref
  1.2 1.3 %reshape.19 = f32[2048]{0:T(1024)} convert(bf16[2048]{0:T(1024)(128)(2,1)} %param.18) | non-fusion elementwise | flops 2048 | bytes 12288 | tf_op jit(solution)/shard_map/reshape | solution.py:432
  2.5 69.6 %shard_map.118 = bf16[8,512]{1,0:T(8,128)(2,1)} custom-call(bf16[8,768]{1,0:T(8,128)(2,1)} %q_ref.1, bf16[8,2048]{1,0:T(8,128)(2,1)} %res_ref.1, s32[8,6]{1,0:T(8,128)} %ids_ref.1, f32[8,6]{1,0:T(8,128)} %mix_ref.1, f32[1,384]{1,0:T(1,128)} %compare_convert_fusion.live_ref, bf16[576,384]{1,0:T(8,128)(2,1)} %bitcast.8, bf16[4,256,128]{2,1,0:T(8,128)(2,1)} %kv_ref.1, ...), custom_call_target="tpu_custom_call" | custom-call | tf_op jit(solution)/shard_map/pallas_call | solution.py:436
  72.1 1.3 %copy.15 = bf16[8,512]{1,0:T(8,128)(2,1)} copy(bf16[8,512]{1,0:T(8,128)(2,1)} %shard_map.118) | data formatting | bytes 16384
where the time goes:
time: 73.7 us; the launch traced here: 73.4 us
  Pallas kernels  69.6 us (94%)
  other arithmetic  1.88 us (3%)
  local copies, waits for them, and re-layouts  1.3 us (2%)
    pallas_call x1, Pallas kernels, fused_body(): pl.pallas_call(functools.partial(fused_kernel, (ctx, sub, tok, heads, exp...  69.6 us

commit v1 on v0

v1 whole, which is shorter than its diff:
```python
import functools

import jax
import jax.numpy as jnp
from jax import lax
from jax.experimental import pallas as pl
from jax.experimental.pallas import tpu as pltpu
from jax.sharding import PartitionSpec as P

D = 2048
NOPE = 128
ROPE = 64
VDIM = 128
LATENT = 512
TOP = 6
CAP = 2


epsilon = 1e-06


def local_attention(absorbed, cache_rows, length, up_value):
    scores = jnp.einsum("qhc,kc->qhk", absorbed, cache_rows, preferred_element_type=jnp.float32) * (
        NOPE + ROPE
    ) ** (-0.5)
    live_mask = lax.broadcasted_iota(jnp.int32, (cache_rows.shape[0],), 0) < length
    scores = jnp.where(live_mask[None, None, :], scores, -jnp.inf)
    highest = jnp.max(scores, axis=2)
    weights = jnp.exp(scores - highest[:, :, None]).astype(jnp.bfloat16)
    totals = jnp.sum(weights, axis=2, dtype=jnp.float32)
    latent_out = jnp.einsum(
        "qhk,kl->qhl", weights, cache_rows[:, :LATENT], preferred_element_type=jnp.float32
    ).astype(jnp.bfloat16)
    head_out = jnp.einsum("qhl,hvl->qhv", latent_out, up_value, preferred_element_type=jnp.float32)
    return (highest, totals, head_out)


def body(
    queries,
    latent_cache,
    cache_len,
    kv_up,
    o_weight,
    residual,
    norm_gain,
    route_ids,
    route_weights,
    w_gate,
    w_up,
    w_down,
):
    ctx_count = lax.axis_size("ctx")
    sub_count = lax.axis_size("sub")
    heads_dev = kv_up.shape[0]
    token_count = queries.shape[0]
    up_full = lax.all_gather(kv_up, "ctx", axis=2, tiled=True)
    up_key = up_full[:, :NOPE, :]
    up_value = up_full[:, NOPE:, :]
    own_rows = queries.reshape(token_count, heads_dev, NOPE + ROPE)
    query_latent = jnp.einsum(
        "qhn,hnl->qhl", own_rows[:, :, :NOPE], up_key, preferred_element_type=jnp.float32
    ).astype(jnp.bfloat16)
    mine = jnp.concatenate([query_latent, own_rows[:, :, NOPE:]], axis=2).reshape(
        token_count, heads_dev * (LATENT + ROPE)
    )
    absorbed = lax.all_gather(mine, "ctx", axis=0, tiled=True).reshape(-1, heads_dev, LATENT + ROPE)
    highest, totals, head_out = local_attention(absorbed, latent_cache, cache_len[0], up_value)
    all_rows = absorbed.shape[0]
    got_out, got_high, got_total = (
        lax.all_to_all(
            head_out.reshape(all_rows, heads_dev * VDIM),
            "ctx",
            split_axis=0,
            concat_axis=0,
            tiled=True,
        ),
        lax.all_to_all(highest, "ctx", split_axis=0, concat_axis=0, tiled=True),
        lax.all_to_all(totals, "ctx", split_axis=0, concat_axis=0, tiled=True),
    )
    got_out = got_out.reshape(ctx_count, token_count, heads_dev, VDIM)
    got_high = got_high.reshape(ctx_count, token_count, heads_dev)
    got_total = got_total.reshape(ctx_count, token_count, heads_dev)
    overall = jnp.max(got_high, axis=0)
    factor = jnp.exp(got_high - overall[None])
    numerator = jnp.sum(got_out * factor[:, :, :, None], axis=0)
    denominator = jnp.sum(got_total * factor, axis=0)
    attention = (
        (numerator / denominator[:, :, None])
        .astype(jnp.bfloat16)
        .reshape(token_count, heads_dev * VDIM)
    )
    projected = jnp.dot(
        attention,
        lax.all_gather(o_weight, "ctx", axis=1, tiled=True),
        preferred_element_type=jnp.float32,
    )
    quarter = D // sub_count
    offset_cols = lax.axis_index("sub") * quarter
    hidden = residual.astype(jnp.float32) + lax.psum(projected.astype(jnp.bfloat16), "sub").astype(
        jnp.float32
    )
    inverse_rms = lax.rsqrt(jnp.mean(hidden * hidden, axis=1) + epsilon)
    normed = (hidden * inverse_rms[:, None] * norm_gain.astype(jnp.float32)).astype(jnp.bfloat16)
    hidden_part = lax.dynamic_slice_in_dim(hidden, offset_cols, quarter, 1)
    experts_dev = w_gate.shape[0]
    expert_total = experts_dev * ctx_count
    pair_count = token_count * TOP
    expert_ids = route_ids.reshape(pair_count)
    onehot = (expert_ids[:, None] == lax.broadcasted_iota(jnp.int32, (1, expert_total), 1)).astype(
        jnp.int32
    )
    earlier = jnp.cumsum(onehot, axis=0) - onehot
    slot_ids = jnp.sum(earlier * onehot, axis=1)
    targets = (expert_ids * CAP + slot_ids).reshape(token_count, TOP)
    matches = targets[:, :, None] == lax.broadcasted_iota(jnp.int32, (1, 1, expert_total * CAP), 2)
    select = jnp.sum(matches.astype(jnp.int32), axis=1).astype(jnp.bfloat16)
    outgoing = jnp.einsum("tj,td->jd", select, normed, preferred_element_type=jnp.float32).astype(
        jnp.bfloat16
    )
    outgoing = outgoing.reshape(ctx_count, experts_dev, CAP, D)
    received = lax.all_to_all(outgoing, "ctx", split_axis=0, concat_axis=0, tiled=True)
    gate_act = jnp.einsum("sekd,edf->sekf", received, w_gate, preferred_element_type=jnp.float32)
    up_act = jnp.einsum("sekd,edf->sekf", received, w_up, preferred_element_type=jnp.float32)
    gated_rows = (jax.nn.silu(gate_act) * up_act).astype(jnp.bfloat16)
    partial_out = jnp.einsum(
        "sekf,efd->sekd", gated_rows, w_down, preferred_element_type=jnp.float32
    )
    summed = lax.psum_scatter(
        partial_out.astype(jnp.bfloat16), "sub", scatter_dimension=3, tiled=True
    )
    back_rows = lax.all_to_all(summed, "ctx", split_axis=0, concat_axis=0, tiled=True)
    back_rows = back_rows.reshape(expert_total * CAP, quarter)
    mixing = jnp.sum(jnp.where(matches, route_weights[:, :, None], 0.0), axis=1)
    routed = jnp.dot(mixing, back_rows.astype(jnp.float32), precision=lax.Precision.HIGHEST)
    return (hidden_part + routed).astype(jnp.bfloat16)


LANES = 128
TILE = 256
CHUNKS = 1
MESH = pl.DeviceIdType.MESH
F32 = jnp.float32
BF16 = jnp.bfloat16
NT = (((1,), (1,)), ((), ()))


def fused_kernel(
    dims,
    q_hbm,
    res_hbm,
    ids_hbm,
    mix_hbm,
    len_hbm,
    cache_hbm,
    kv_hbm,
    o_hbm,
    gain_hbm,
    gate_hbm,
    up_hbm,
    down_hbm,
    out_ref,
    res_ref,
    ids_ref,
    mix_ref,
    len_ref,
    cache_ref,
    kv_ref,
    o_ref,
    gain_ref,
    q_all,
    res_all,
    comb_send,
    comb_all,
    ql_all,
    lat_send,
    lat_all,
    stat_all,
    att_all,
    proj_send,
    proj_all,
    hid_all,
    normed,
    mix_cols,
    gated,
    fin_send,
    fin_all,
    gate_buf,
    up_buf,
    down_buf,
    in_sem,
    w_sem,
    ctx_send,
    ctx_recv,
    comb_ssem,
    comb_rsem,
    sub_send,
    sub_recv,
    hid_ssem,
    hid_rsem,
    fin_ssem,
    fin_rsem,
):
    grp, ctx, sub, tok, heads, experts = dims
    me_g = lax.axis_index("grp")
    me_c = lax.axis_index("ctx")
    me_s = lax.axis_index("sub")
    span = ctx * tok
    rows = heads * span
    chunk = rows // CHUNKS
    chunk_heads = heads // CHUNKS
    quarter = o_ref.shape[1]
    hidden_units = gate_hbm.shape[1]

    barrier = pltpu.get_barrier_semaphore()

    def everyone():
        for dg in range(grp):
            for dc in range(ctx):
                for ds in range(sub):
                    if dg or dc or ds:
                        yield (
                            (dg * ctx + dc) * sub + ds,
                            lax.rem(me_g + dg, grp),
                            lax.rem(me_c + dc, ctx),
                            lax.rem(me_s + ds, sub),
                        )

    for _, pg, pc, ps in everyone():
        pl.semaphore_signal(
            barrier,
            inc=1,
            device_id={"grp": pg, "ctx": pc, "sub": ps},
            device_id_type=MESH,
        )

    loads = [
        pltpu.make_async_copy(source, target, in_sem.at[i])
        for i, (source, target) in enumerate(
            (
                (q_hbm, q_all.at[me_c]),
                (kv_hbm, kv_ref),
                (res_hbm, res_ref),
                (ids_hbm, ids_ref),
                (mix_hbm, mix_ref),
                (len_hbm, len_ref),
                (cache_hbm, cache_ref),
                (o_hbm, o_ref),
                (gain_hbm, gain_ref),
            )
        )
    ]
    q_load, kv_load, res_load, ids_load, mix_load, len_load, cache_load, o_load, gain_load = loads
    for load in loads:
        load.start()

    weight_loads = []
    for e in range(experts):
        place = pl.ds(e * hidden_units, hidden_units)
        for i, (source, target) in enumerate(
            ((gate_hbm, gate_buf), (up_hbm, up_buf), (down_hbm, down_buf))
        ):
            weight_loads.append(
                pltpu.make_async_copy(
                    source.at[me_g * experts + e], target.at[place], w_sem.at[e, i]
                )
            )
            weight_loads[-1].start()

    def ctx_copies(phase, source_of, target):
        copies = []
        for d in range(1, ctx):
            peer = lax.rem(me_c + d, ctx)
            copies.append(
                pltpu.make_async_remote_copy(
                    src_ref=source_of(peer),
                    dst_ref=target,
                    send_sem=ctx_send.at[phase, d],
                    recv_sem=ctx_recv.at[phase, d],
                    device_id={"ctx": peer},
                    device_id_type=MESH,
                )
            )
            copies[-1].start()
        return copies

    def finish(copies):
        for copy in copies:
            copy.wait()

    q_load.wait()
    pl.semaphore_wait(barrier, grp * ctx * sub - 1)

    q_copies = ctx_copies(0, lambda peer: q_all.at[me_c], q_all.at[me_c])

    res_load.wait()
    piece = quarter // sub

    def own_piece(peer):
        return pl.ds(pl.multiple_of(peer * quarter + me_s * piece, piece), piece)

    early = ctx_copies(1, lambda peer: res_ref.at[:, own_piece(peer)], res_all.at[me_c])
    res_all[me_c] = res_ref[:, own_piece(me_c)]

    ids_load.wait()
    mix_load.wait()
    lane = lax.broadcasted_iota(jnp.int32, (tok, LANES), 1)
    ids, mixes = ids_ref[...], mix_ref[...]
    for c in range(ctx):
        for g in range(grp):
            first = (c * grp + g) * experts
            comb = jnp.zeros((tok, LANES), F32)
            for k in range(TOP):
                hit = (ids[:, k : k + 1] == lane + first) & (lane < experts)
                comb += jnp.where(hit, mixes[:, k : k + 1], 0.0)
            comb_send[g * ctx + c] = comb
    comb_all[me_g * ctx + me_c] = comb_send[me_g * ctx + me_c]
    for dg in range(grp):
        for dc in range(ctx):
            if dg or dc:
                pg, pc = lax.rem(me_g + dg, grp), lax.rem(me_c + dc, ctx)
                early.append(
                    pltpu.make_async_remote_copy(
                        src_ref=comb_send.at[pg * ctx + pc],
                        dst_ref=comb_all.at[me_g * ctx + me_c],
                        send_sem=comb_ssem.at[dg * ctx + dc],
                        recv_sem=comb_rsem.at[dg * ctx + dc],
                        device_id={"grp": pg, "ctx": pc},
                        device_id_type=MESH,
                    )
                )
                early[-1].start()

    kv_load.wait()
    finish(q_copies)
    per_head = NOPE + ROPE
    q_rows = q_all[...].astype(F32).reshape(span, heads * per_head)
    turned = [
        q_rows if h == 0 else pltpu.roll(q_rows, (heads - h) * per_head, 1) for h in range(heads)
    ]
    ql_copies = []
    for k in range(CHUNKS):
        for h in range(k * chunk_heads, (k + 1) * chunk_heads):
            nope = turned[h][:, :NOPE].astype(BF16)
            part = jnp.dot(nope, kv_ref[h, :NOPE, :], preferred_element_type=F32).astype(BF16)
            ql_all[me_c, h * span : (h + 1) * span, :] = part
        block = ql_all.at[me_c, pl.ds(k * chunk, chunk)]
        ql_copies.append(ctx_copies(2 + k, lambda peer: block, block))

    cache_load.wait()
    len_load.wait()
    position = lax.broadcasted_iota(jnp.int32, (1, cache_ref.shape[1]), 1)
    live = position < len_ref[0]
    rope_scores = []
    for k in range(CHUNKS):
        rope = jnp.concatenate(
            [
                turned[h][:, NOPE:per_head]
                for h in range(k * chunk_heads, (k + 1) * chunk_heads)
            ],
            axis=0,
        ).astype(BF16)
        rope_scores.append(jnp.dot(rope, cache_ref[LATENT:, :], preferred_element_type=F32))

    lat_copies = []
    for k in range(CHUNKS):
        finish(ql_copies[k])
        part = slice(k * chunk, (k + 1) * chunk)
        lat_q = jnp.concatenate([ql_all[c, part, :] for c in range(ctx)], axis=1)
        scores = jnp.dot(lat_q, cache_ref[:LATENT, :], preferred_element_type=F32)
        scores = (scores + rope_scores[k]) * (NOPE + ROPE) ** (-0.5)
        scores = jnp.where(live, scores, -jnp.inf)
        highest = jnp.max(scores, axis=1, keepdims=True)
        weights = jnp.exp(scores - highest).astype(BF16)
        latent = lax.dot_general(
            weights, cache_ref[:LATENT, :], NT, preferred_element_type=F32
        ).astype(BF16)
        for c in range(ctx):
            lat_send[c, part, :] = latent[:, c * LANES : (c + 1) * LANES]
        block = pl.ds(k * chunk, chunk)
        copies = ctx_copies(
            2 + CHUNKS + k,
            lambda peer: lat_send.at[peer, block],
            lat_all.at[me_c, block],
        )
        lat_all[me_c, part, :] = lat_send[me_c, part, :]
        totals = jnp.sum(weights.astype(F32), axis=1, keepdims=True)
        side = lax.broadcasted_iota(jnp.int32, (chunk, LANES), 1)
        stats = jnp.where(side < 4, highest, totals).T
        stat_all[me_c, k] = stats[0:8, :]
        copies += ctx_copies(
            2 + 2 * CHUNKS + k, lambda peer: stat_all.at[me_c, k], stat_all.at[me_c, k]
        )
        lat_copies.append(copies)

    att_copies = []
    for k in range(CHUNKS):
        finish(lat_copies[k])
        part = slice(k * chunk, (k + 1) * chunk)
        highs = [stat_all[c, k, 0:1, :] for c in range(ctx)]
        overall = functools.reduce(jnp.maximum, highs)
        factors = [jnp.exp(high - overall) for high in highs]
        denominator = sum(f * stat_all[c, k, 4:5, :] for c, f in enumerate(factors))
        merged = jnp.zeros((chunk, LANES), F32)
        for c in range(ctx):
            scale = jnp.broadcast_to(factors[c] / denominator, (LANES, chunk)).T
            merged += lat_all[c, part, :].astype(F32) * scale
        merged = merged.astype(BF16)
        for j in range(chunk_heads):
            h = k * chunk_heads + j
            out = lax.dot_general(
                merged[j * span : (j + 1) * span, :],
                kv_ref[h, NOPE:, :],
                NT,
                preferred_element_type=F32,
            )
            att_all[me_c, k, :, j * VDIM : (j + 1) * VDIM] = out.astype(BF16)
        block = att_all.at[me_c, k]
        att_copies.append(ctx_copies(2 + 3 * CHUNKS + k, lambda peer: block, block))

    o_load.wait()
    width = chunk_heads * VDIM
    projected = jnp.zeros((span, quarter), F32)
    for k in range(CHUNKS):
        finish(att_copies[k])
        attention = sum(att_all[c, k].astype(F32) for c in range(ctx)).astype(BF16)
        projected += jnp.dot(
            attention, o_ref[k * width : (k + 1) * width, :], preferred_element_type=F32
        )
    for s in range(sub):
        proj_send[s] = projected[:, s * piece : (s + 1) * piece].astype(BF16)
    copies = []
    for d in range(1, sub):
        peer = lax.rem(me_s + d, sub)
        copies.append(
            pltpu.make_async_remote_copy(
                src_ref=proj_send.at[peer],
                dst_ref=proj_all.at[me_s],
                send_sem=sub_send.at[d],
                recv_sem=sub_recv.at[d],
                device_id={"sub": peer},
                device_id_type=MESH,
            )
        )
        copies[-1].start()
    proj_all[me_s] = proj_send[me_s]
    finish(early)

    comb = comb_all[...].reshape(grp * span, LANES)
    comb_lane = lax.broadcasted_iota(jnp.int32, (grp * span, LANES), 1)
    columns = [
        jnp.sum(jnp.where(comb_lane == e, comb, 0.0), axis=1, keepdims=True)
        for e in range(experts)
    ]
    for t in range(experts * hidden_units // LANES):
        low, high = t * LANES // hidden_units, (t * LANES + LANES - 1) // hidden_units
        mix = jnp.broadcast_to(columns[low], (grp * span, LANES))
        if high > low:
            mix = jnp.where(comb_lane < high * hidden_units - t * LANES, mix, columns[high])
        mix_cols[:, t * LANES : (t + 1) * LANES] = mix

    residual = res_all[...].astype(F32).reshape(span, piece)
    finish(copies)
    me = (me_g * ctx + me_c) * sub + me_s
    hid_all[me] = (residual + sum(proj_all[s].astype(F32) for s in range(sub))).astype(BF16)
    copies = []
    for i, pg, pc, ps in everyone():
        copies.append(
            pltpu.make_async_remote_copy(
                src_ref=hid_all.at[me],
                dst_ref=hid_all.at[me],
                send_sem=hid_ssem.at[i],
                recv_sem=hid_rsem.at[i],
                device_id={"grp": pg, "ctx": pc, "sub": ps},
                device_id_type=MESH,
            )
        )
        copies[-1].start()
    gain_load.wait()
    gain = gain_ref[...].astype(F32)
    finish(copies)

    parts = ctx * sub
    for g in range(grp):
        own = slice(g * span, (g + 1) * span)
        pieces = [hid_all[g * parts + j].astype(F32) for j in range(parts)]
        squares = jnp.sum(sum(p * p for p in pieces), axis=1, keepdims=True)
        inverse_rms = lax.rsqrt(squares / (parts * piece) + epsilon)
        for j in range(parts):
            normed[own, j * piece : (j + 1) * piece] = (
                pieces[j] * inverse_rms * gain[j : j + 1, :]
            ).astype(BF16)

    finish(weight_loads)
    for t in range(experts * hidden_units // TILE):
        tile = slice(t * TILE, (t + 1) * TILE)
        gate_act = lax.dot_general(gate_buf[tile, :], normed[...], NT, preferred_element_type=F32)
        up_act = lax.dot_general(up_buf[tile, :], normed[...], NT, preferred_element_type=F32)
        both = gate_act / (1.0 + jnp.exp(-gate_act)) * up_act
        gated[:, tile] = (both.T * mix_cols[:, tile]).astype(BF16)

    copies = []
    for ds in range(sub):
        ps = lax.rem(me_s + ds, sub)
        cols = pl.ds(pl.multiple_of(ps * quarter, quarter), quarter)
        block = jnp.dot(gated[...], down_buf[:, cols], preferred_element_type=F32).astype(BF16)
        for i in range(grp * ctx):
            fin_send[ds, i] = block[i * tok : (i + 1) * tok, :]
        for dg in range(grp):
            for dc in range(ctx):
                pg, pc = lax.rem(me_g + dg, grp), lax.rem(me_c + dc, ctx)
                if dg or dc or ds:
                    i = (dg * ctx + dc) * sub + ds
                    copies.append(
                        pltpu.make_async_remote_copy(
                            src_ref=fin_send.at[ds, pg * ctx + pc],
                            dst_ref=fin_all.at[me],
                            send_sem=fin_ssem.at[i],
                            recv_sem=fin_rsem.at[i],
                            device_id={"grp": pg, "ctx": pc, "sub": ps},
                            device_id_type=MESH,
                        )
                    )
                    copies[-1].start()
        if ds == 0:
            fin_all[me] = fin_send[0, me_g * ctx + me_c]
    hidden = jnp.concatenate(
        [
            hid_all[(me_g * ctx + me_s) * sub + s].astype(F32)
            for s in range(sub)
        ],
        axis=1,
    )
    mine = jnp.zeros((tok, quarter), F32)
    for c in range(ctx):
        mine += jnp.where(me_c == c, hidden[c * tok : (c + 1) * tok, :], 0.0)
    finish(copies)
    routed = sum(fin_all[i].astype(F32) for i in range(grp * ctx * sub))
    out_ref[...] = (mine + routed).astype(out_ref.dtype)


def fused_body(
    queries,
    latent_cache,
    cache_len,
    kv_up,
    o_weight,
    residual,
    norm_gain,
    route_ids,
    route_weights,
    w_gate,
    w_up,
    w_down,
):
    grp, ctx, sub = lax.axis_size("grp"), lax.axis_size("ctx"), lax.axis_size("sub")
    heads, tok, experts = kv_up.shape[0], queries.shape[0], w_gate.shape[0] // grp
    span, rows, quarter = ctx * tok, heads * ctx * tok, o_weight.shape[1]
    width, piece, everyone = residual.shape[1], quarter // sub, grp * ctx * sub
    w_gate, w_up = jnp.swapaxes(w_gate, 1, 2), jnp.swapaxes(w_up, 1, 2)
    units = experts * w_gate.shape[1]
    cache = latent_cache.T
    gain = norm_gain.reshape(width // LANES, LANES)
    hbm = pl.BlockSpec(memory_space=pl.ANY)
    dma = pltpu.SemaphoreType.DMA
    return pl.pallas_call(
        functools.partial(fused_kernel, (grp, ctx, sub, tok, heads, experts)),
        out_shape=jax.ShapeDtypeStruct((tok, width // sub), BF16),
        in_specs=[hbm] * 12,
        out_specs=pl.BlockSpec(memory_space=pltpu.VMEM),
        scratch_shapes=[
            pltpu.VMEM(residual.shape, BF16),
            pltpu.VMEM(route_ids.shape, jnp.int32),
            pltpu.VMEM(route_weights.shape, F32),
            pltpu.SMEM(cache_len.shape, jnp.int32),
            pltpu.VMEM(cache.shape, BF16),
            pltpu.VMEM(kv_up.shape, BF16),
            pltpu.VMEM(o_weight.shape, BF16),
            pltpu.VMEM(gain.shape, BF16),
            pltpu.VMEM((ctx,) + queries.shape, BF16),
            pltpu.VMEM((ctx, tok, piece), BF16),
            pltpu.VMEM((grp * ctx, tok, LANES), F32),
            pltpu.VMEM((grp * ctx, tok, LANES), F32),
            pltpu.VMEM((ctx, rows, LANES), BF16),
            pltpu.VMEM((ctx, rows, LANES), BF16),
            pltpu.VMEM((ctx, rows, LANES), BF16),
            pltpu.VMEM((ctx, CHUNKS, 8, rows // CHUNKS), F32),
            pltpu.VMEM((ctx, CHUNKS, span, heads * VDIM // CHUNKS), BF16),
            pltpu.VMEM((sub, span, piece), BF16),
            pltpu.VMEM((sub, span, piece), BF16),
            pltpu.VMEM((everyone, span, piece), BF16),
            pltpu.VMEM((grp * span, width), BF16),
            pltpu.VMEM((grp * span, units), F32),
            pltpu.VMEM((grp * span, units), BF16),
            pltpu.VMEM((sub, grp * ctx, tok, quarter), BF16),
            pltpu.VMEM((everyone, tok, quarter), BF16),
            pltpu.VMEM((units, width), BF16),
            pltpu.VMEM((units, width), BF16),
            pltpu.VMEM((units, width), BF16),
            dma((9,)),
            dma((experts, 3)),
            dma((2 + 4 * CHUNKS, ctx)),
            dma((2 + 4 * CHUNKS, ctx)),
            dma((grp * ctx,)),
            dma((grp * ctx,)),
            dma((sub,)),
            dma((sub,)),
            dma((everyone,)),
            dma((everyone,)),
            dma((everyone,)),
            dma((everyone,)),
        ],
        compiler_params=pltpu.CompilerParams(
            collective_id=0, has_side_effects=True, vmem_limit_bytes=56 * 1024 * 1024
        ),
    )(
        queries,
        residual,
        route_ids,
        route_weights,
        cache_len,
        cache,
        kv_up,
        o_weight,
        gain,
        w_gate,
        w_up,
        w_down,
    )


def choose_body(*args):
    kv_up, o_weight, w_gate = args[3], args[4], args[9]
    grp, ctx, sub = lax.axis_size("grp"), lax.axis_size("ctx"), lax.axis_size("sub")
    tok, experts = args[0].shape[0], w_gate.shape[0]
    units = experts // grp * w_gate.shape[2]
    fits = (
        ctx == sub
        and kv_up.shape[2] == LANES
        and o_weight.shape[1] == sub * LANES
        and kv_up.shape[0] * ctx * tok == LANES
        and experts % grp == 0
        and experts <= LANES
        and w_gate.shape[2] % 16 == 0
        and units % TILE == 0
        and units * w_gate.shape[1] * 6 <= 40 * 1024 * 1024
        and tok % 8 == 0
    )
    return fused_body(*args) if fits else body(*args)


def solution(mesh):
    in_specs = (
        P(("grp", "ctx"), "sub"),
        P(("grp", "ctx"), None),
        P(("grp", "ctx")),
        P(("grp", "sub"), None, "ctx"),
        P("sub", "ctx"),
        P(("grp", "ctx"), None),
        P(),
        P(("grp", "ctx"), None),
        P(("grp", "ctx"), None),
        P("ctx", None, "sub"),
        P("ctx", None, "sub"),
        P("ctx", "sub", None),
    )
    out_specs = P(("grp", "ctx"), "sub")
    return jax.shard_map(choose_body, mesh=mesh, in_specs=in_specs, out_specs=out_specs, check_vma=False)
```

time: 73.7 us -> 60 us (0.81)
  Pallas kernels: 69.6 us -> 57.8 us
  other arithmetic: 1.88 us -> 0 us
    pallas_call x1, Pallas kernels: 69.6 us -> 57.8 us  [fused_body(): pl.pallas_call(functools.partial(fused_kernel, (grp, ctx, sub, tok, heads...]
    reshape x1 -> x0, other arithmetic: 1.29 us -> none  [fused_body(): gain = norm_gain.astype(F32).reshape(1, width)]
where the time goes in v1:
time: 60 us; the launch traced here: 59.7 us
  Pallas kernels  57.8 us (96%)
  local copies, waits for them, and re-layouts  1.3 us (2%)
  between operations  0.66 us (1%)
    pallas_call x1, Pallas kernels, fused_body(): pl.pallas_call(functools.partial(fused_kernel, (grp, ctx, sub, tok, heads...  57.8 us
    unnamed x1, local copies, waits for them, and re-layouts  1.3 us

profile of v1, /device:TPU:0, one launch (start us, length us, event | category | flops | bytes accessed | tf_op | source)
XLA Modules:
  0.0 59.7 jit_solution(345294376086723198)
XLA Ops:
  0.7 57.8 %shard_map.118 = bf16[8,512]{1,0:T(8,128)(2,1)} custom-call(bf16[8,768]{1,0:T(8,128)(2,1)} %q_hbm.1, bf16[8,2048]{1,0:T(8,128)(2,1)} %res_hbm.1, s32[8,6]{1,0:T(8,128)} %ids_hbm.1, f32[8,6]{1,0:T(8,128)} %mix_hbm.1, s32[1]{0:T(128)S(6)} %copy.14.len_hbm, bf16[576,384]{1,0:T(8,128)(2,1)} %bitcast.6, bf16[4,256,128]{2,1,0:T(8,128)(2,1)} %kv_hbm.1, ...), custom_call_target="tpu_custom_call" | custom-call | tf_op jit(solution)/shard_map/pallas_call | solution.py:565
  58.4 1.3 %copy.15 = bf16[8,512]{1,0:T(8,128)(2,1)} copy(bf16[8,512]{1,0:T(8,128)(2,1)} %shard_map.118) | data formatting | bytes 16384

commit v2 on v1

--- a/solution.py
+++ b/solution.py
@@ -179,9 +179,14 @@
     proj_send,
     proj_all,
     hid_all,
-    normed,
+    gain_rows,
+    tokens,
+    gate_sum,
+    up_sum,
     mix_cols,
     gated,
+    pair_send,
+    pair_all,
     fin_send,
     fin_all,
     gate_buf,
@@ -197,6 +202,8 @@
     sub_recv,
     hid_ssem,
     hid_rsem,
+    pair_ssem,
+    pair_rsem,
     fin_ssem,
     fin_rsem,
 ):
@@ -264,33 +271,61 @@
                     source.at[me_g * experts + e], target.at[place], w_sem.at[e, i]
                 )
             )
-            weight_loads[-1].start()
-
-    def ctx_copies(phase, source_of, target):
-        copies = []
-        for d in range(1, ctx):
-            peer = lax.rem(me_c + d, ctx)
-            copies.append(
-                pltpu.make_async_remote_copy(
-                    src_ref=source_of(peer),
-                    dst_ref=target,
-                    send_sem=ctx_send.at[phase, d],
-                    recv_sem=ctx_recv.at[phase, d],
-                    device_id={"ctx": peer},
-                    device_id_type=MESH,
-                )
+            weight_loads[-1].start(priority=1)
+
+    upper = me_c // (ctx // 2)
+    sends = []
+
+    def far(i):
+        low = ctx - 1 - i
+        low = low - (me_c - low + ctx) // ctx
+        high = i + (i - me_c + ctx) // ctx
+        return low + upper * (high - low)
+
+    far_first = [far(i) for i in range(ctx - 1)]
+    near_first = far_first[::-1]
+
+    def send(source, target, send_sem, recv_sem, **peer):
+        copy = pltpu.make_async_remote_copy(
+            src_ref=source,
+            dst_ref=target,
+            send_sem=send_sem,
+            recv_sem=recv_sem,
+            device_id=peer,
+            device_id_type=MESH,
+        )
+        copy.start()
+        sends.append(copy)
+
+    def arrived(target, recv_sem):
+        pltpu.make_async_remote_copy(
+            src_ref=target,
+            dst_ref=target,
+            send_sem=sub_send.at[0],
+            recv_sem=recv_sem,
+            device_id={"ctx": far_first[0]},
+            device_id_type=MESH,
+        ).wait_recv()
+
+    def ctx_copies(phase, source_of, target_of):
+        for i, peer in enumerate(far_first):
+            send(
+                source_of(peer),
+                target_of(me_c),
+                ctx_send.at[phase, i],
+                ctx_recv.at[phase, me_c],
+                ctx=peer,
             )
-            copies[-1].start()
-        return copies
-
-    def finish(copies):
-        for copy in copies:
-            copy.wait()
+        return [(target_of(peer), ctx_recv.at[phase, peer]) for peer in near_first]
+
+    def finish(arrivals):
+        for arrival in arrivals:
+            arrived(*arrival)
 
     q_load.wait()
     pl.semaphore_wait(barrier, grp * ctx * sub - 1)
 
-    q_copies = ctx_copies(0, lambda peer: q_all.at[me_c], q_all.at[me_c])
+    q_copies = ctx_copies(0, lambda peer: q_all.at[me_c], lambda c: q_all.at[c])
 
     res_load.wait()
     piece = quarter // sub
@@ -298,7 +333,9 @@
     def own_piece(peer):
         return pl.ds(pl.multiple_of(peer * quarter + me_s * piece, piece), piece)
 
-    early = ctx_copies(1, lambda peer: res_ref.at[:, own_piece(peer)], res_all.at[me_c])
+    early = ctx_copies(
+        1, lambda peer: res_ref.at[:, own_piece(peer)], lambda c: res_all.at[c]
+    )
     res_all[me_c] = res_ref[:, own_piece(me_c)]
 
     ids_load.wait()
@@ -314,21 +351,19 @@
                 comb += jnp.where(hit, mixes[:, k : k + 1], 0.0)
             comb_send[g * ctx + c] = comb
     comb_all[me_g * ctx + me_c] = comb_send[me_g * ctx + me_c]
+    me_gc = me_g * ctx + me_c
     for dg in range(grp):
-        for dc in range(ctx):
-            if dg or dc:
-                pg, pc = lax.rem(me_g + dg, grp), lax.rem(me_c + dc, ctx)
-                early.append(
-                    pltpu.make_async_remote_copy(
-                        src_ref=comb_send.at[pg * ctx + pc],
-                        dst_ref=comb_all.at[me_g * ctx + me_c],
-                        send_sem=comb_ssem.at[dg * ctx + dc],
-                        recv_sem=comb_rsem.at[dg * ctx + dc],
-                        device_id={"grp": pg, "ctx": pc},
-                        device_id_type=MESH,
-                    )
-                )
-                early[-1].start()
+        pg = lax.rem(me_g + dg, grp)
+        for i, pc in enumerate(far_first if dg == 0 else far_first + [me_c]):
+            send(
+                comb_send.at[pg * ctx + pc],
+                comb_all.at[me_gc],
+                comb_ssem.at[dg * ctx + i],
+                comb_rsem.at[me_gc],
+                grp=pg,
+                ctx=pc,
+            )
+            early.append((comb_all.at[pg * ctx + pc], comb_rsem.at[pg * ctx + pc]))
 
     kv_load.wait()
     finish(q_copies)
@@ -343,8 +378,10 @@
             nope = turned[h][:, :NOPE].astype(BF16)
             part = jnp.dot(nope, kv_ref[h, :NOPE, :], preferred_element_type=F32).astype(BF16)
             ql_all[me_c, h * span : (h + 1) * span, :] = part
-        block = ql_all.at[me_c, pl.ds(k * chunk, chunk)]
-        ql_copies.append(ctx_copies(2 + k, lambda peer: block, block))
+        block = pl.ds(k * chunk, chunk)
+        ql_copies.append(
+            ctx_copies(2 + k, lambda peer: ql_all.at[me_c, block], lambda c: ql_all.at[c, block])
+        )
 
     cache_load.wait()
     len_load.wait()
@@ -380,7 +417,7 @@
         copies = ctx_copies(
             2 + CHUNKS + k,
             lambda peer: lat_send.at[peer, block],
-            lat_all.at[me_c, block],
+            lambda c: lat_all.at[c, block],
         )
         lat_all[me_c, part, :] = lat_send[me_c, part, :]
         totals = jnp.sum(weights.astype(F32), axis=1, keepdims=True)
@@ -388,7 +425,7 @@
         stats = jnp.where(side < 4, highest, totals).T
         stat_all[me_c, k] = stats[0:8, :]
         copies += ctx_copies(
-            2 + 2 * CHUNKS + k, lambda peer: stat_all.at[me_c, k], stat_all.at[me_c, k]
+            2 + 2 * CHUNKS + k, lambda peer: stat_all.at[me_c, k], lambda c: stat_all.at[c, k]
         )
         lat_copies.append(copies)
 
@@ -414,8 +451,11 @@
                 preferred_element_type=F32,
             )
             att_all[me_c, k, :, j * VDIM : (j + 1) * VDIM] = out.astype(BF16)
-        block = att_all.at[me_c, k]
-        att_copies.append(ctx_copies(2 + 3 * CHUNKS + k, lambda peer: block, block))
+        att_copies.append(
+            ctx_copies(
+                2 + 3 * CHUNKS + k, lambda peer: att_all.at[me_c, k], lambda c: att_all.at[c, k]
+            )
+        )
 
     o_load.wait()
     width = chunk_heads * VDIM
@@ -431,19 +471,12 @@
     copies = []
     for d in range(1, sub):
         peer = lax.rem(me_s + d, sub)
-        copies.append(
-            pltpu.make_async_remote_copy(
-                src_ref=proj_send.at[peer],
-                dst_ref=proj_all.at[me_s],
-                send_sem=sub_send.at[d],
-                recv_sem=sub_recv.at[d],
-                device_id={"sub": peer},
-                device_id_type=MESH,
-            )
-        )
-        copies[-1].start()
+        send(proj_send.at[peer], proj_all.at[me_s], sub_send.at[d], sub_recv.at[me_s], sub=peer)
+        copies.append((proj_all.at[peer], sub_recv.at[peer]))
     proj_all[me_s] = proj_send[me_s]
     finish(early)
+    gain_load.wait()
+    gain_rows[...] = gain_ref[...].astype(F32)
 
     comb = comb_all[...].reshape(grp * span, LANES)
     comb_lane = lax.broadcasted_iota(jnp.int32, (grp * span, LANES), 1)
@@ -462,80 +495,121 @@
     finish(copies)
     me = (me_g * ctx + me_c) * sub + me_s
     hid_all[me] = (residual + sum(proj_all[s].astype(F32) for s in range(sub))).astype(BF16)
-    copies = []
-    for i, pg, pc, ps in everyone():
-        copies.append(
-            pltpu.make_async_remote_copy(
-                src_ref=hid_all.at[me],
-                dst_ref=hid_all.at[me],
-                send_sem=hid_ssem.at[i],
-                recv_sem=hid_rsem.at[i],
-                device_id={"grp": pg, "ctx": pc, "sub": ps},
-                device_id_type=MESH,
+    count = 0
+    for k in range(ctx):
+        pc = me_c if k == 0 else near_first[k - 1]
+        for dg in range(grp):
+            for ds in range(sub):
+                if k or dg or ds:
+                    send(
+                        hid_all.at[me],
+                        hid_all.at[me],
+                        hid_ssem.at[count],
+                        hid_rsem.at[me],
+                        grp=lax.rem(me_g + dg, grp),
+                        ctx=pc,
+                        sub=lax.rem(me_s + ds, sub),
+                    )
+                    count += 1
+
+    for load in weight_loads:
+        load.wait()
+    squares = [jnp.zeros((span, piece), F32) for _ in range(grp)]
+    tiles = experts * hidden_units // TILE
+    for k in range(ctx):
+        pc = me_c if k == 0 else near_first[k - 1]
+        for dg in range(grp):
+            for ds in range(sub):
+                if k or dg or ds:
+                    at = (lax.rem(me_g + dg, grp) * ctx + pc) * sub + lax.rem(me_s + ds, sub)
+                    arrived(hid_all.at[at], hid_rsem.at[at])
+        for g in range(grp):
+            for t in range(sub):
+                block = hid_all[(g * ctx + pc) * sub + t].astype(F32)
+                squares[g] += block * block
+                scaled = block * gain_rows[pl.ds(pc * sub + t, 1), :]
+                tokens[k, g * span : (g + 1) * span, t * piece : (t + 1) * piece] = scaled.astype(
+                    BF16
+                )
+        if k == ctx - 1:
+            means = jnp.sum(jnp.concatenate(squares, axis=0), axis=1, keepdims=True) / (
+                ctx * quarter
             )
-        )
-        copies[-1].start()
-    gain_load.wait()
-    gain = gain_ref[...].astype(F32)
-    finish(copies)
-
-    parts = ctx * sub
-    for g in range(grp):
-        own = slice(g * span, (g + 1) * span)
-        pieces = [hid_all[g * parts + j].astype(F32) for j in range(parts)]
-        squares = jnp.sum(sum(p * p for p in pieces), axis=1, keepdims=True)
-        inverse_rms = lax.rsqrt(squares / (parts * piece) + epsilon)
-        for j in range(parts):
-            normed[own, j * piece : (j + 1) * piece] = (
-                pieces[j] * inverse_rms * gain[j : j + 1, :]
-            ).astype(BF16)
-
-    finish(weight_loads)
-    for t in range(experts * hidden_units // TILE):
-        tile = slice(t * TILE, (t + 1) * TILE)
-        gate_act = lax.dot_general(gate_buf[tile, :], normed[...], NT, preferred_element_type=F32)
-        up_act = lax.dot_general(up_buf[tile, :], normed[...], NT, preferred_element_type=F32)
-        both = gate_act / (1.0 + jnp.exp(-gate_act)) * up_act
-        gated[:, tile] = (both.T * mix_cols[:, tile]).astype(BF16)
-
-    copies = []
-    for ds in range(sub):
-        ps = lax.rem(me_s + ds, sub)
-        cols = pl.ds(pl.multiple_of(ps * quarter, quarter), quarter)
-        block = jnp.dot(gated[...], down_buf[:, cols], preferred_element_type=F32).astype(BF16)
+            inverse_rms = jnp.broadcast_to(lax.rsqrt(means + epsilon), (grp * span, LANES)).T[:1, :]
+        cols = pl.ds(pl.multiple_of(pc * quarter, quarter), quarter)
+        for t in range(tiles):
+            tile = slice(t * TILE, (t + 1) * TILE)
+            gate_act = lax.dot_general(
+                gate_buf[tile, cols], tokens[k], NT, preferred_element_type=F32
+            )
+            up_act = lax.dot_general(up_buf[tile, cols], tokens[k], NT, preferred_element_type=F32)
+            if k > 0:
+                gate_act += gate_sum[tile, :]
+                up_act += up_sum[tile, :]
+            if k < ctx - 1:
+                gate_sum[tile, :] = gate_act
+                up_sum[tile, :] = up_act
+            else:
+                gate_act *= inverse_rms
+                both = gate_act / (1.0 + jnp.exp(-gate_act)) * (up_act * inverse_rms)
+                gated[:, tile] = (both.T * mix_cols[:, tile]).astype(BF16)
+
+    pairs = sub // 2
+    me_p, side = me_s // 2, lax.rem(me_s, 2)
+
+    def down(s):
+        cols = pl.ds(pl.multiple_of(s * quarter, quarter), quarter)
+        return jnp.dot(gated[...], down_buf[:, cols], preferred_element_type=F32)
+
+    turns = [lax.rem(me_p + dp, pairs) for dp in range(1, pairs)] + [me_p]
+    for n, pp in enumerate(turns):
+        pair_send[n] = down(2 * pp + 1 - side).astype(BF16)
+        send(
+            pair_send.at[n],
+            pair_all.at[pp],
+            pair_ssem.at[n],
+            pair_rsem.at[pp],
+            sub=2 * me_p + 1 - side,
+        )
+    arrivals = []
+    me_half = me_gc * pairs + me_p
+    for n, pp in enumerate(turns):
+        block = down(2 * pp + side)
+        arrived(pair_all.at[pp], pair_rsem.at[pp])
+        block = (block + pair_all[pp].astype(F32)).astype(BF16)
         for i in range(grp * ctx):
-            fin_send[ds, i] = block[i * tok : (i + 1) * tok, :]
-        for dg in range(grp):
-            for dc in range(ctx):
-                pg, pc = lax.rem(me_g + dg, grp), lax.rem(me_c + dc, ctx)
-                if dg or dc or ds:
-                    i = (dg * ctx + dc) * sub + ds
-                    copies.append(
-                        pltpu.make_async_remote_copy(
-                            src_ref=fin_send.at[ds, pg * ctx + pc],
-                            dst_ref=fin_all.at[me],
-                            send_sem=fin_ssem.at[i],
-                            recv_sem=fin_rsem.at[i],
-                            device_id={"grp": pg, "ctx": pc, "sub": ps},
-                            device_id_type=MESH,
-                        )
-                    )
-                    copies[-1].start()
-        if ds == 0:
-            fin_all[me] = fin_send[0, me_g * ctx + me_c]
+            fin_send[n, i] = block[i * tok : (i + 1) * tok, :]
+        count = 0
+        for pc in far_first + [me_c]:
+            for dg in range(grp):
+                pg = lax.rem(me_g + dg, grp)
+                if pc is me_c and dg == 0 and n == pairs - 1:
+                    fin_all[me_half] = fin_send[n, me_gc]
+                    continue
+                send(
+                    fin_send.at[n, pg * ctx + pc],
+                    fin_all.at[me_half],
+                    fin_ssem.at[n * grp * ctx + count],
+                    fin_rsem.at[me_half],
+                    grp=pg,
+                    ctx=pc,
+                    sub=2 * pp + side,
+                )
+                count += 1
+                at = (pg * ctx + pc) * pairs + pp
+                arrivals.append((fin_all.at[at], fin_rsem.at[at]))
     hidden = jnp.concatenate(
-        [
-            hid_all[(me_g * ctx + me_s) * sub + s].astype(F32)
-            for s in range(sub)
-        ],
+        [hid_all[(me_g * ctx + me_s) * sub + t].astype(F32) for t in range(sub)],
         axis=1,
     )
     mine = jnp.zeros((tok, quarter), F32)
     for c in range(ctx):
         mine += jnp.where(me_c == c, hidden[c * tok : (c + 1) * tok, :], 0.0)
-    finish(copies)
-    routed = sum(fin_all[i].astype(F32) for i in range(grp * ctx * sub))
+    finish(arrivals)
+    routed = sum(fin_all[i].astype(F32) for i in range(grp * ctx * pairs))
     out_ref[...] = (mine + routed).astype(out_ref.dtype)
+    for copy in sends:
+        copy.wait_send()
 
 
 def fused_body(
@@ -588,11 +662,16 @@
             pltpu.VMEM((sub, span, piece), BF16),
             pltpu.VMEM((sub, span, piece), BF16),
             pltpu.VMEM((everyone, span, piece), BF16),
-            pltpu.VMEM((grp * span, width), BF16),
+            pltpu.VMEM(gain.shape, F32),
+            pltpu.VMEM((ctx, grp * span, quarter), BF16),
+            pltpu.VMEM((units, grp * span), F32),
+            pltpu.VMEM((units, grp * span), F32),
             pltpu.VMEM((grp * span, units), F32),
             pltpu.VMEM((grp * span, units), BF16),
-            pltpu.VMEM((sub, grp * ctx, tok, quarter), BF16),
-            pltpu.VMEM((everyone, tok, quarter), BF16),
+            pltpu.VMEM((sub // 2, grp * span, quarter), BF16),
+            pltpu.VMEM((sub // 2, grp * span, quarter), BF16),
+            pltpu.VMEM((sub // 2, grp * ctx, tok, quarter), BF16),
+            pltpu.VMEM((everyone // 2, tok, quarter), BF16),
             pltpu.VMEM((units, width), BF16),
             pltpu.VMEM((units, width), BF16),
             pltpu.VMEM((units, width), BF16),
@@ -606,8 +685,10 @@
             dma((sub,)),
             dma((everyone,)),
             dma((everyone,)),
-            dma((everyone,)),
-            dma((everyone,)),
+            dma((sub // 2,)),
+            dma((sub // 2,)),
+            dma((everyone // 2,)),
+            dma((everyone // 2,)),
         ],
         compiler_params=pltpu.CompilerParams(
             collective_id=0, has_side_effects=True, vmem_limit_bytes=56 * 1024 * 1024
@@ -635,6 +716,7 @@
     units = experts // grp * w_gate.shape[2]
     fits = (
         ctx == sub
+        and ctx % 2 == 0
         and kv_up.shape[2] == LANES
         and o_weight.shape[1] == sub * LANES
         and kv_up.shape[0] * ctx * tok == LANES

time: 60 us -> 51.2 us (0.85)
  Pallas kernels: 57.8 us -> 49 us
    pallas_call x1, Pallas kernels: 57.8 us -> 49 us  [fused_body(): pl.pallas_call(functools.partial(fused_kernel, (grp, ctx, sub, tok, heads...]
where the time goes in v2:
time: 51.2 us; the launch traced here: 51 us
  Pallas kernels  49 us (96%)
  local copies, waits for them, and re-layouts  1.3 us (3%)
  between operations  0.66 us (1%)
    pallas_call x1, Pallas kernels, fused_body(): pl.pallas_call(functools.partial(fused_kernel, (grp, ctx, sub, tok, heads...  49 us
    unnamed x1, local copies, waits for them, and re-layouts  1.3 us

profile of v2, /device:TPU:0, one launch (start us, length us, event | category | flops | bytes accessed | tf_op | source)
XLA Modules:
  0.0 51.0 jit_solution(13997454495457214093)
XLA Ops:
  0.7 49.0 %shard_map.118 = bf16[8,512]{1,0:T(8,128)(2,1)} custom-call(bf16[8,768]{1,0:T(8,128)(2,1)} %q_hbm.1, bf16[8,2048]{1,0:T(8,128)(2,1)} %res_hbm.1, s32[8,6]{1,0:T(8,128)} %ids_hbm.1, f32[8,6]{1,0:T(8,128)} %mix_hbm.1, s32[1]{0:T(128)S(6)} %copy.14.len_hbm, bf16[576,384]{1,0:T(8,128)(2,1)} %bitcast.6, bf16[4,256,128]{2,1,0:T(8,128)(2,1)} %kv_hbm.1, ...), custom_call_target="tpu_custom_call" | custom-call | tf_op jit(solution)/shard_map/pallas_call | solution.py:639
  49.7 1.3 %copy.15 = bf16[8,512]{1,0:T(8,128)(2,1)} copy(bf16[8,512]{1,0:T(8,128)(2,1)} %shard_map.118) | data formatting | bytes 16384

commit v3 on v2

--- a/solution.py
+++ b/solution.py
@@ -495,22 +495,36 @@
     finish(copies)
     me = (me_g * ctx + me_c) * sub + me_s
     hid_all[me] = (residual + sum(proj_all[s].astype(F32) for s in range(sub))).astype(BF16)
-    count = 0
-    for k in range(ctx):
-        pc = me_c if k == 0 else near_first[k - 1]
+    def spread(pc, k):
+        slot = (me_g * ctx + pc) * sub + me_s
+        count = 0
         for dg in range(grp):
             for ds in range(sub):
-                if k or dg or ds:
+                if dg or ds:
                     send(
-                        hid_all.at[me],
-                        hid_all.at[me],
-                        hid_ssem.at[count],
-                        hid_rsem.at[me],
+                        hid_all.at[slot],
+                        hid_all.at[slot],
+                        hid_ssem.at[k * grp * sub + count],
+                        hid_rsem.at[slot],
                         grp=lax.rem(me_g + dg, grp),
-                        ctx=pc,
                         sub=lax.rem(me_s + ds, sub),
                     )
                     count += 1
+
+    for i, pc in enumerate(far_first):
+        send(
+            hid_all.at[me],
+            hid_all.at[me],
+            hid_ssem.at[i * grp * sub + grp * sub - 1],
+            hid_rsem.at[me],
+            ctx=pc,
+        )
+    spread(me_c, 0)
+
+    def relay(k):
+        slot = (me_g * ctx + near_first[k - 1]) * sub + me_s
+        arrived(hid_all.at[slot], hid_rsem.at[slot])
+        spread(near_first[k - 1], k)
 
     for load in weight_loads:
         load.wait()
@@ -520,7 +534,7 @@
         pc = me_c if k == 0 else near_first[k - 1]
         for dg in range(grp):
             for ds in range(sub):
-                if k or dg or ds:
+                if dg or ds:
                     at = (lax.rem(me_g + dg, grp) * ctx + pc) * sub + lax.rem(me_s + ds, sub)
                     arrived(hid_all.at[at], hid_rsem.at[at])
         for g in range(grp):
@@ -538,6 +552,10 @@
             inverse_rms = jnp.broadcast_to(lax.rsqrt(means + epsilon), (grp * span, LANES)).T[:1, :]
         cols = pl.ds(pl.multiple_of(pc * quarter, quarter), quarter)
         for t in range(tiles):
+            if k == 0:
+                for ahead in range(1, ctx):
+                    if t == (ahead - 1) * tiles // ctx:
+                        relay(ahead)
             tile = slice(t * TILE, (t + 1) * TILE)
             gate_act = lax.dot_general(
                 gate_buf[tile, cols], tokens[k], NT, preferred_element_type=F32
@@ -636,9 +654,9 @@
     gain = norm_gain.reshape(width // LANES, LANES)
     hbm = pl.BlockSpec(memory_space=pl.ANY)
     dma = pltpu.SemaphoreType.DMA
-    return pl.pallas_call(
+    out = pl.pallas_call(
         functools.partial(fused_kernel, (grp, ctx, sub, tok, heads, experts)),
-        out_shape=jax.ShapeDtypeStruct((tok, width // sub), BF16),
+        out_shape=jax.ShapeDtypeStruct((tok, width // sub), F32),
         in_specs=[hbm] * 12,
         out_specs=pl.BlockSpec(memory_space=pltpu.VMEM),
         scratch_shapes=[
@@ -691,22 +709,30 @@
             dma((everyone // 2,)),
         ],
         compiler_params=pltpu.CompilerParams(
-            collective_id=0, has_side_effects=True, vmem_limit_bytes=56 * 1024 * 1024
+            collective_id=0, has_side_effects=True, vmem_limit_bytes=46 * 1024 * 1024
         ),
     )(
-        queries,
-        residual,
-        route_ids,
-        route_weights,
-        cache_len,
-        cache,
-        kv_up,
-        o_weight,
-        gain,
-        w_gate,
-        w_up,
-        w_down,
-    )
+        *(
+            operand
+            if operand is cache_len
+            else pltpu.with_memory_space_constraint(operand, pltpu.HBM)
+            for operand in (
+                queries,
+                residual,
+                route_ids,
+                route_weights,
+                cache_len,
+                cache,
+                kv_up,
+                o_weight,
+                gain,
+                w_gate,
+                w_up,
+                w_down,
+            )
+        )
+    )
+    return out.astype(BF16)
 
 
 def choose_body(*args):

time: 51.2 us -> 49.2 us (0.961)
  local copies, waits for them, and re-layouts: 1.3 us -> 0 us
  Pallas kernels: 49 us -> 47.7 us
  other arithmetic: 0 us -> 0.6 us
    unnamed x1 -> x0, local copies, waits for them, and re-layouts: 1.3 us -> none
    pallas_call x1, Pallas kernels: 49 us -> 47.7 us  [fused_body(): pl.pallas_call(functools.partial(fused_kernel, (grp, ctx, sub, tok, heads...]
    convert_element_type x0 -> x1, other arithmetic: none -> 0.6 us  [fused_body(): return out.astype(BF16)]
where the time goes in v3:
time: 49.2 us; the launch traced here: 49 us
  Pallas kernels  47.7 us (97%)
  between operations  0.66 us (1%)
  other arithmetic  0.6 us (1%)
    pallas_call x1, Pallas kernels, fused_body(): pl.pallas_call(functools.partial(fused_kernel, (grp, ctx, sub, tok, heads...  47.7 us

profile of v3, /device:TPU:0, one launch (start us, length us, event | category | flops | bytes accessed | tf_op | source)
XLA Modules:
  0.0 49.0 jit_solution(8987996020456142959)
XLA Ops:
  0.7 47.7 %shard_map.118 = f32[8,512]{1,0:T(8,128)S(1)} custom-call(bf16[8,768]{1,0:T(8,128)(2,1)} %q_hbm.1, bf16[8,2048]{1,0:T(8,128)(2,1)} %res_hbm.1, s32[8,6]{1,0:T(8,128)} %ids_hbm.1, f32[8,6]{1,0:T(8,128)} %mix_hbm.1, s32[1]{0:T(128)S(6)} %copy.13.len_hbm, bf16[576,384]{1,0:T(8,128)(2,1)} %bitcast.6, bf16[4,256,128]{2,1,0:T(8,128)(2,1)} %kv_hbm.1, ...), custom_call_target="tpu_custom_call" | custom-call | tf_op jit(solution)/shard_map/pallas_call | solution.py:657
  48.4 0.6 %convert_element_type.3 = bf16[8,512]{1,0:T(8,128)(2,1)} convert(f32[8,512]{1,0:T(8,128)S(1)} %shard_map.118) | non-fusion elementwise | flops 4096 | bytes 24576 | tf_op jit(solution)/shard_map/convert_element_type | solution.py:735

commit v4 on v3

--- a/solution.py
+++ b/solution.py
@@ -232,14 +232,6 @@
                             lax.rem(me_s + ds, sub),
                         )
 
-    for _, pg, pc, ps in everyone():
-        pl.semaphore_signal(
-            barrier,
-            inc=1,
-            device_id={"grp": pg, "ctx": pc, "sub": ps},
-            device_id_type=MESH,
-        )
-
     loads = [
         pltpu.make_async_copy(source, target, in_sem.at[i])
         for i, (source, target) in enumerate(
@@ -260,18 +252,40 @@
     for load in loads:
         load.start()
 
+    for _, pg, pc, ps in everyone():
+        pl.semaphore_signal(
+            barrier,
+            inc=1,
+            device_id={"grp": pg, "ctx": pc, "sub": ps},
+            device_id_type=MESH,
+        )
+
     weight_loads = []
-    for e in range(experts):
-        place = pl.ds(e * hidden_units, hidden_units)
-        for i, (source, target) in enumerate(
-            ((gate_hbm, gate_buf), (up_hbm, up_buf), (down_hbm, down_buf))
-        ):
+    for i, (source, target) in enumerate(
+        ((gate_hbm, gate_buf), (up_hbm, up_buf), (down_hbm, down_buf))
+    ):
+        for e in range(experts):
+            place = pl.ds(e * hidden_units, hidden_units)
             weight_loads.append(
                 pltpu.make_async_copy(
                     source.at[me_g * experts + e], target.at[place], w_sem.at[e, i]
                 )
             )
             weight_loads[-1].start(priority=1)
+    tiles = experts * hidden_units // TILE
+
+    def turn_tiles(buffer, loads, first=0, last=tiles):
+        for load in loads:
+            load.wait()
+
+        def turn(t, carry):
+            place = pl.ds(pl.multiple_of(t * TILE, TILE), TILE)
+            for j in range(buffer.shape[1] // TILE):
+                cols = slice(j * TILE, (j + 1) * TILE)
+                buffer[place, cols] = buffer[place, cols].T
+            return carry
+
+        lax.fori_loop(first, last, turn, 0)
 
     upper = me_c // (ctx // 2)
     sends = []
@@ -398,6 +412,7 @@
         ).astype(BF16)
         rope_scores.append(jnp.dot(rope, cache_ref[LATENT:, :], preferred_element_type=F32))
 
+    turn_tiles(gate_buf, weight_loads[:experts], 0, 2 * tiles // 3)
     lat_copies = []
     for k in range(CHUNKS):
         finish(ql_copies[k])
@@ -429,6 +444,8 @@
         )
         lat_copies.append(copies)
 
+    turn_tiles(gate_buf, [], 2 * tiles // 3)
+    turn_tiles(up_buf, weight_loads[experts : 2 * experts], 0, tiles // 3)
     att_copies = []
     for k in range(CHUNKS):
         finish(lat_copies[k])
@@ -457,6 +474,7 @@
             )
         )
 
+    turn_tiles(up_buf, [], tiles // 3)
     o_load.wait()
     width = chunk_heads * VDIM
     projected = jnp.zeros((span, quarter), F32)
@@ -526,10 +544,9 @@
         arrived(hid_all.at[slot], hid_rsem.at[slot])
         spread(near_first[k - 1], k)
 
-    for load in weight_loads:
+    for load in weight_loads[2 * experts :]:
         load.wait()
     squares = [jnp.zeros((span, piece), F32) for _ in range(grp)]
-    tiles = experts * hidden_units // TILE
     for k in range(ctx):
         pc = me_c if k == 0 else near_first[k - 1]
         for dg in range(grp):
@@ -549,28 +566,39 @@
             means = jnp.sum(jnp.concatenate(squares, axis=0), axis=1, keepdims=True) / (
                 ctx * quarter
             )
-            inverse_rms = jnp.broadcast_to(lax.rsqrt(means + epsilon), (grp * span, LANES)).T[:1, :]
-        cols = pl.ds(pl.multiple_of(pc * quarter, quarter), quarter)
+            inverse_rms = lax.rsqrt(means + epsilon)
+        halves = quarter // TILE
+        cols = [
+            pl.ds(pl.multiple_of(pc * quarter + n * TILE, TILE), TILE) for n in range(halves)
+        ]
         for t in range(tiles):
             if k == 0:
                 for ahead in range(1, ctx):
                     if t == (ahead - 1) * tiles // ctx:
                         relay(ahead)
             tile = slice(t * TILE, (t + 1) * TILE)
-            gate_act = lax.dot_general(
-                gate_buf[tile, cols], tokens[k], NT, preferred_element_type=F32
-            )
-            up_act = lax.dot_general(up_buf[tile, cols], tokens[k], NT, preferred_element_type=F32)
+
+            def product(buffer):
+                return sum(
+                    jnp.dot(
+                        tokens[k, :, n * TILE : (n + 1) * TILE],
+                        buffer[tile, cols[n]],
+                        preferred_element_type=F32,
+                    )
+                    for n in range(halves)
+                )
+
+            gate_act, up_act = product(gate_buf), product(up_buf)
             if k > 0:
-                gate_act += gate_sum[tile, :]
-                up_act += up_sum[tile, :]
+                gate_act += gate_sum[:, tile]
+                up_act += up_sum[:, tile]
             if k < ctx - 1:
-                gate_sum[tile, :] = gate_act
-                up_sum[tile, :] = up_act
+                gate_sum[:, tile] = gate_act
+                up_sum[:, tile] = up_act
             else:
                 gate_act *= inverse_rms
                 both = gate_act / (1.0 + jnp.exp(-gate_act)) * (up_act * inverse_rms)
-                gated[:, tile] = (both.T * mix_cols[:, tile]).astype(BF16)
+                gated[:, tile] = (both * mix_cols[:, tile]).astype(BF16)
 
     pairs = sub // 2
     me_p, side = me_s // 2, lax.rem(me_s, 2)
@@ -682,8 +710,8 @@
             pltpu.VMEM((everyone, span, piece), BF16),
             pltpu.VMEM(gain.shape, F32),
             pltpu.VMEM((ctx, grp * span, quarter), BF16),
-            pltpu.VMEM((units, grp * span), F32),
-            pltpu.VMEM((units, grp * span), F32),
+            pltpu.VMEM((grp * span, units), F32),
+            pltpu.VMEM((grp * span, units), F32),
             pltpu.VMEM((grp * span, units), F32),
             pltpu.VMEM((grp * span, units), BF16),
             pltpu.VMEM((sub // 2, grp * span, quarter), BF16),
@@ -750,6 +778,7 @@
         and experts <= LANES
         and w_gate.shape[2] % 16 == 0
         and units % TILE == 0
+        and o_weight.shape[1] % TILE == 0
         and units * w_gate.shape[1] * 6 <= 40 * 1024 * 1024
         and tok % 8 == 0
     )

time: 49.2 us -> 47.3 us (0.961)
  Pallas kernels: 47.7 us -> 45.8 us
    pallas_call x1, Pallas kernels: 47.7 us -> 45.8 us  [fused_body(): pl.pallas_call(functools.partial(fused_kernel, (grp, ctx, sub, tok, heads...]
where the time goes in v4:
time: 47.3 us; the launch traced here: 47.1 us
  Pallas kernels  45.8 us (97%)
  between operations  0.66 us (1%)
  other arithmetic  0.6 us (1%)
    pallas_call x1, Pallas kernels, fused_body(): pl.pallas_call(functools.partial(fused_kernel, (grp, ctx, sub, tok, heads...  45.8 us

profile of v4, /device:TPU:0, one launch (start us, length us, event | category | flops | bytes accessed | tf_op | source)
XLA Modules:
  0.0 47.1 jit_solution(11924954754100670697)
XLA Ops:
  0.7 45.8 %shard_map.118 = f32[8,512]{1,0:T(8,128)S(1)} custom-call(bf16[8,768]{1,0:T(8,128)(2,1)} %q_hbm.1, bf16[8,2048]{1,0:T(8,128)(2,1)} %res_hbm.1, s32[8,6]{1,0:T(8,128)} %ids_hbm.1, f32[8,6]{1,0:T(8,128)} %mix_hbm.1, s32[1]{0:T(128)S(6)} %copy.13.len_hbm, bf16[576,384]{1,0:T(8,128)(2,1)} %bitcast.6, bf16[4,256,128]{2,1,0:T(8,128)(2,1)} %kv_hbm.1, ...), custom_call_target="tpu_custom_call" | custom-call | tf_op jit(solution)/shard_map/pallas_call | solution.py:685
  46.5 0.6 %convert_element_type.3 = bf16[8,512]{1,0:T(8,128)(2,1)} convert(f32[8,512]{1,0:T(8,128)S(1)} %shard_map.118) | non-fusion elementwise | flops 4096 | bytes 24576 | tf_op jit(solution)/shard_map/convert_element_type | solution.py:763

commit v5 on v4

--- a/solution.py
+++ b/solution.py
@@ -187,6 +187,7 @@
     gated,
     pair_send,
     pair_all,
+    own_sum,
     fin_send,
     fin_all,
     gate_buf,
@@ -620,9 +621,9 @@
     arrivals = []
     me_half = me_gc * pairs + me_p
     for n, pp in enumerate(turns):
-        block = down(2 * pp + side)
+        own_sum[n] = down(2 * pp + side)
         arrived(pair_all.at[pp], pair_rsem.at[pp])
-        block = (block + pair_all[pp].astype(F32)).astype(BF16)
+        block = (own_sum[n] + pair_all[pp].astype(F32)).astype(BF16)
         for i in range(grp * ctx):
             fin_send[n, i] = block[i * tok : (i + 1) * tok, :]
         count = 0
@@ -651,11 +652,11 @@
     mine = jnp.zeros((tok, quarter), F32)
     for c in range(ctx):
         mine += jnp.where(me_c == c, hidden[c * tok : (c + 1) * tok, :], 0.0)
+    for copy in sends:
+        copy.wait_send()
     finish(arrivals)
     routed = sum(fin_all[i].astype(F32) for i in range(grp * ctx * pairs))
     out_ref[...] = (mine + routed).astype(out_ref.dtype)
-    for copy in sends:
-        copy.wait_send()
 
 
 def fused_body(
@@ -716,6 +717,7 @@
             pltpu.VMEM((grp * span, units), BF16),
             pltpu.VMEM((sub // 2, grp * span, quarter), BF16),
             pltpu.VMEM((sub // 2, grp * span, quarter), BF16),
+            pltpu.VMEM((sub // 2, grp * span, quarter), F32),
             pltpu.VMEM((sub // 2, grp * ctx, tok, quarter), BF16),
             pltpu.VMEM((everyone // 2, tok, quarter), BF16),
             pltpu.VMEM((units, width), BF16),

time: 47.3 us -> 46.8 us (0.989)
    pallas_call x1, Pallas kernels: 45.8 us -> 45.4 us  [fused_body(): pl.pallas_call(functools.partial(fused_kernel, (grp, ctx, sub, tok, heads...]
where the time goes in v5:
time: 46.8 us; the launch traced here: 46.6 us
  Pallas kernels  45.4 us (97%)
  between operations  0.66 us (1%)
  other arithmetic  0.6 us (1%)
    pallas_call x1, Pallas kernels, fused_body(): pl.pallas_call(functools.partial(fused_kernel, (grp, ctx, sub, tok, heads...  45.4 us

profile of v5, /device:TPU:0, one launch (start us, length us, event | category | flops | bytes accessed | tf_op | source)
XLA Modules:
  0.0 46.6 jit_solution(11505153396349610302)
XLA Ops:
  0.7 45.4 %shard_map.118 = f32[8,512]{1,0:T(8,128)S(1)} custom-call(bf16[8,768]{1,0:T(8,128)(2,1)} %q_hbm.1, bf16[8,2048]{1,0:T(8,128)(2,1)} %res_hbm.1, s32[8,6]{1,0:T(8,128)} %ids_hbm.1, f32[8,6]{1,0:T(8,128)} %mix_hbm.1, s32[1]{0:T(128)S(6)} %copy.13.len_hbm, bf16[576,384]{1,0:T(8,128)(2,1)} %bitcast.6, bf16[4,256,128]{2,1,0:T(8,128)(2,1)} %kv_hbm.1, ...), custom_call_target="tpu_custom_call" | custom-call | tf_op jit(solution)/shard_map/pallas_call | solution.py:686
  46.0 0.6 %convert_element_type.3 = bf16[8,512]{1,0:T(8,128)(2,1)} convert(f32[8,512]{1,0:T(8,128)S(1)} %shard_map.118) | non-fusion elementwise | flops 4096 | bytes 24576 | tf_op jit(solution)/shard_map/convert_element_type | solution.py:765
